TPU v7x, 32 devices: a whole 2x2x4 slice. The times are simulated.
32 devices in a mesh: blk: 2 (over y), uly: 4 (over x, core), dp: 4 (over z).
Axes of the slice: x: 2, y: 2, z: 4, core: 2. Of those that a mesh axis runs over, the one named last changes fastest.
Arguments:
- tokens: bfloat16 [1024, 4096], P(('uly', 'dp')), may hold values from -6 to 6
- expert_ids: int32 [1024, 8], P(('uly', 'dp')), may hold values from 0 to 15, all different within a row; in each aligned block of 64 rows (0 to 63, 64 to 127, ...) at most 40 rows name the same one
- route_weight: float32 [1024, 8], P(('uly', 'dp')), may hold values from 0.05 to 0.5
- w_gate: bfloat16 [16, 4096, 1024], P(('uly', 'dp'), None, 'blk'), may hold values from -0.09375 to 0.09375
- w_up: bfloat16 [16, 4096, 1024], P(('uly', 'dp'), None, 'blk'), may hold values from -0.09375 to 0.09375
- w_down: bfloat16 [16, 1024, 4096], P(('uly', 'dp'), 'blk'), may hold values from -0.1875 to 0.1875
Outputs:
- mixed: bfloat16 [1024, 4096], P(('uly', 'dp'), 'blk')
Inputs may be any that keep to these rules, and one draw needn't show every extreme that they name: `expert_ids`: each row names 8 different experts. In each aligned block of 64 rows (the rows of one device) no expert is named by more than 40 rows, and in some block one expert is named by exactly 40 rows.
All inputs are finite; a program needn't handle non-finite values.
Results may differ from a plain program's by a relative error of at most 0.015.
Values may be sent and summed in bfloat16 or wider, within the bound.
A program may use at most 64 MiB of HBM per device.

v0:
```python
import jax
import jax.numpy as jnp
from jax import lax
from jax.sharding import PartitionSpec as P


def routing_tables(expert_ids, route_weight, groups, local_count, capacity):
    tokens_here, picks_count = expert_ids.shape
    experts = groups * local_count
    labels = lax.broadcasted_iota(jnp.int32, (1, 1, experts), 2)
    onehot = (expert_ids[:, :, None] == labels).astype(jnp.int32)
    chosen = jnp.sum(onehot, axis=1)
    before = jnp.cumsum(chosen, axis=0) - chosen
    slot_of = jnp.sum(onehot * before[:, None, :], axis=2)
    places = lax.broadcasted_iota(jnp.int32, (1, 1, capacity), 2)
    slot_hot = (slot_of[:, :, None] == places).astype(jnp.float32)
    expert_hot = onehot.astype(jnp.float32).reshape(tokens_here, picks_count, groups, local_count)
    placing = jnp.einsum("tkgl,tkc->gclt", expert_hot, slot_hot)
    placing = placing.reshape(groups * capacity * local_count, tokens_here)
    mixing = jnp.einsum("tkgl,tkc,tk->tgcl", expert_hot, slot_hot, route_weight)
    mixing = mixing.reshape(tokens_here, groups * capacity * local_count)
    return (placing.astype(jnp.bfloat16), mixing)


def local(tokens, expert_ids, route_weight, w_gate, w_up, w_down):
    ulysses_size = lax.axis_size("uly")
    data_size = lax.axis_size("dp")
    cycle_size = lax.axis_size("blk")
    tokens_here, model_width = tokens.shape
    local_count = w_gate.shape[0]
    hidden_cut = w_gate.shape[2]
    groups = ulysses_size * data_size
    experts = groups * local_count
    picks_count = expert_ids.shape[1]
    capacity = min(tokens_here, max(2, 5 * tokens_here * picks_count // (4 * experts)))
    placing, mixing = routing_tables(expert_ids, route_weight, groups, local_count, capacity)
    slice_width = model_width // cycle_size
    rows_total = groups * capacity
    cycle_index = lax.axis_index("blk")
    own_part = lax.dynamic_slice_in_dim(tokens, cycle_index * slice_width, slice_width, 1)
    outgoing = jnp.dot(placing, own_part, preferred_element_type=jnp.float32).astype(jnp.bfloat16)
    outgoing = outgoing.reshape(ulysses_size, data_size, capacity, local_count, slice_width)
    arrived = lax.all_to_all(
        lax.all_to_all(outgoing, "uly", split_axis=0, concat_axis=0, tiled=True),
        "dp",
        split_axis=1,
        concat_axis=1,
        tiled=True,
    )
    arrived = arrived.reshape(rows_total, local_count, slice_width)
    portion = lax.all_gather(arrived, "blk", axis=2, tiled=True)
    gate_more = jnp.einsum("rlw,lwf->rlf", portion, w_gate, preferred_element_type=jnp.float32)
    up_more = jnp.einsum("rlw,lwf->rlf", portion, w_up, preferred_element_type=jnp.float32)
    hidden = (jax.nn.silu(gate_more) * up_more).astype(jnp.bfloat16)
    resplit = lax.all_to_all(w_down, "blk", split_axis=2, concat_axis=1, tiled=True)
    zero_sum = jnp.zeros((slice_width, rows_total * local_count), jnp.float32)
    total = zero_sum
    portion = lax.all_gather(hidden, "blk", axis=2, tiled=True)
    ranges_count = portion.shape[2] // hidden_cut
    for number in range(ranges_count):
        part_hidden = portion[:, :, number * hidden_cut : (number + 1) * hidden_cut]
        part_rows = lax.dynamic_slice_in_dim(resplit, number * hidden_cut, hidden_cut, 1)
        partial_value = jnp.einsum(
            "lfd,rlf->drl", part_rows, part_hidden, preferred_element_type=jnp.float32
        )
        partial_value = partial_value.reshape(slice_width, rows_total * local_count)
        total = total + partial_value.astype(jnp.bfloat16).astype(jnp.float32)
    returned = total.astype(jnp.bfloat16).reshape(
        slice_width, ulysses_size, data_size, capacity, local_count
    )
    returned_rows = lax.all_to_all(
        lax.all_to_all(returned, "uly", split_axis=1, concat_axis=1, tiled=True),
        "dp",
        split_axis=2,
        concat_axis=2,
        tiled=True,
    )
    returned_rows = returned_rows.reshape(slice_width, rows_total * local_count).astype(jnp.float32)
    mixed = lax.dot_general(
        mixing, returned_rows, (((1,), (1,)), ((), ())), precision=lax.Precision.HIGHEST
    )
    return mixed.astype(jnp.bfloat16)


def solution(mesh):
    return jax.shard_map(
        local,
        mesh=mesh,
        in_specs=(
            P(("uly", "dp"), None),
            P(("uly", "dp"), None),
            P(("uly", "dp"), None),
            P(("uly", "dp"), None, "blk"),
            P(("uly", "dp"), None, "blk"),
            P(("uly", "dp"), "blk", None),
        ),
        out_specs=P(("uly", "dp"), "blk"),
        check_vma=False,
    )
```

profile of v0, /device:TPU:18, one launch (start us, length us, event | category | flops | bytes accessed | tf_op | source)
XLA Modules:
  0.0 366.6 jit_solution(7828955031235225768)
XLA Ops:
  6.5 0.0 copy-start
  6.5 0.0 all-gather.3.cloned.1.call-start
  6.5 0.8 copy.29
  7.4 0.2 convert_reduce_fusion
  7.5 0.1 reduce_window_sum.11
  7.6 1.2 select_reduce_fusion
  8.9 0.5 fusion.26
  9.4 0.3 copy.32
  9.7 0.0 copy-done
  9.7 0.8 convolution_convert_fusion.2
  10.5 32.7 %all_to_all.38 = bf16[4,4,40,1,2048]{4,2,1,3,0:T(8,128)(2,1)S(1)} all-to-all(bf16[4,4,40,1,2048]{4,2,1,3,0:T(8,128)(2,1)S(1)} %bitcast.90), channel_id=1, replica_groups=mesh['blk'=2,'uly'=4,'dp'=4] {'uly'}, dimensions={0} | all-to-all | bytes 5242880 | tf_op jit(solution)/shard_map/all_to_all | solution.py:44
  43.3 0.3 copy.34
  43.6 62.0 %all_to_all.39 = bf16[4,4,40,1,2048]{4,2,0,3,1:T(8,128)(2,1)S(1)} all-to-all(bf16[4,4,40,1,2048]{4,2,0,3,1:T(8,128)(2,1)S(1)} %copy.34), channel_id=1, replica_groups=mesh['blk'=2,'uly'=4,'dp'=4] {'dp'}, dimensions={1} | all-to-all | bytes 5242880 | tf_op jit(solution)/shard_map/all_to_all | solution.py:43
  105.6 1.8 copy.35
  107.4 0.0 all-gather.3.cloned.1.call-update
  107.4 19.2 %copy.36 = bf16[1,512,4096]{1,0,2:T(2,128)(2,1)} copy(bf16[1,512,4096]{2,1,0:T(8,128)(2,1)} %param.11) | data formatting | bytes 8388608 | tf_op args[5]
  126.6 0.5 broadcast.24
  127.1 28.5 %reduce = bf16[4096,512]{1,0:T(8,128)(2,1)} reduce(bf16[4096,1,512]{2,1,0:T(2,128)(2,1)} %bitcast.86, bf16[]{:T(256)} %broadcast.24), dimensions={1}, to_apply=%bitcast.81.reduce_sub_computation | reduce | bytes 8388610
  155.6 5.9 %reshape.119 = bf16[2,2,524288]{2,1,0:T(2,128)(2,1)} reshape(bf16[4096,512]{1,0:T(8,128)(2,1)} %reduce) | data formatting | bytes 8388608
  161.5 5.6 %all-to-all-start.2 = ((bf16[2,2,524288]{2,1,0:T(2,128)(2,1)}), bf16[2,2,524288]{2,1,0:T(2,128)(2,1)}, u32[]{:S(2)}, u32[]{:S(2)}) async-start(bf16[2,2,524288]{2,1,0:T(2,128)(2,1)} %reshape.119), calls=%async_computation.2 | async-start | bytes 8388608 | tf_op jit(solution)/shard_map/all_to_all | solution.py:55
  167.1 0.2 all-gather.5.cloned.1.call-start
  167.3 18.0 %all-gather.3.cloned.1.call-done = bf16[640,1,4096]{2,0,1:T(8,128)(2,1)} async-done(((bf16[640,1,2048]{2,0,1:T(8,128)(2,1)}), bf16[640,1,4096]{2,0,1:T(8,128)(2,1)}) %all-gather.3.cloned.1.call-update) | async-done | bytes 5242896 | tf_op jit(solution)/shard_map/all_gather | solution.py:51
  185.3 0.0 copy-start.4
  185.3 0.0 copy-start.5
  185.3 6.2 %fusion.6 = f32[640,1,512]{2,0,1:T(8,128)S(1)} fusion(bf16[1,4096,512]{2,1,0:T(8,128)(2,1)} %param.9, bf16[640,1,4096]{2,0,1:T(8,128)(2,1)} %all-gather.3.cloned.1.call-done), kind=kOutput, calls=%fused_computation.13 | convolution fusion | flops 2684354560 | bytes 10747904 | tf_op jit(solution)/shard_map/rlw,lwf->rlf/dot_general | solution.py:52
  191.5 0.0 copy-done.4
  191.5 0.3 copy-done.5
  191.8 3.9 %fusion.21 = bf16[640,1,512]{2,0,1:T(8,128)(2,1)} fusion(bf16[1,4096,512]{2,1,0:T(8,128)(2,1)S(1)} %copy-done.5, bf16[640,1,4096]{2,0,1:T(8,128)(2,1)S(1)} %copy-done.4, f32[640,1,512]{2,0,1:T(8,128)S(1)} %fusion.6), kind=kOutput, calls=%fused_computation.16 | convolution fusion | flops 2686320640 | bytes 11403264 | tf_op jit(solution)/shard_map/rlw,lwf->rlf/dot_general | solution.py:53
  195.6 0.0 all-gather.5.cloned.1.call-update
  195.7 40.6 %all-to-all-done.2 = bf16[2,2,524288]{2,1,0:T(2,128)(2,1)} async-done(((bf16[2,2,524288]{2,1,0:T(2,128)(2,1)}), bf16[2,2,524288]{2,1,0:T(2,128)(2,1)}, u32[]{:S(2)}, u32[]{:S(2)}) %all-to-all-start.2) | async-done | bytes 4194336 | tf_op jit(solution)/shard_map/all_to_all | solution.py:55
  236.2 7.1 %reshape.120 = bf16[4096,1,512]{2,1,0:T(2,128)(2,1)} reshape(bf16[2,2,524288]{2,1,0:T(2,128)(2,1)} %all-to-all-done.2) | data formatting | bytes 8388608
  243.3 6.6 %copy.41 = bf16[1,512,4096]{1,2,0:T(8,128)(2,1)} copy(bf16[1,512,4096]{1,0,2:T(2,128)(2,1)} %bitcast.87) | data formatting | bytes 8388608
  249.9 6.3 %copy.37 = bf16[1,2,512,2048]{3,2,1,0:T(8,128)(2,1)} copy(bf16[1,2,512,2048]{2,3,1,0:T(8,128)(2,1)} %bitcast.88) | data formatting | bytes 8388608 | tf_op jit(solution)/shard_map/all_to_all | solution.py:55
  256.2 0.0 all-gather.5.cloned.1.call-done
  256.2 0.0 copy-start.2
  256.2 0.0 copy-start.6
  256.2 3.5 convolution_convert_fusion
  259.7 0.0 copy-done.2
  259.7 0.0 copy-done.6
  259.7 1.5 add_convert_fusion
  261.2 32.7 %all_to_all.40 = bf16[2048,4,4,40,1]{0,3,2,4,1:T(8,128)(2,1)S(1)} all-to-all(bf16[2048,4,4,40,1]{0,3,2,4,1:T(8,128)(2,1)S(1)} %bitcast.94), channel_id=1, replica_groups=mesh['blk'=2,'uly'=4,'dp'=4] {'uly'}, dimensions={1} | all-to-all | bytes 5242880 | tf_op jit(solution)/shard_map/all_to_all | solution.py:72
  294.0 1.8 copy.39
  295.8 0.0 copy-start.3
  295.8 5.2 %all-to-all-start.4 = ((bf16[2048,4,4,40,1]{0,3,1,4,2:T(8,128)(2,1)}), bf16[2048,4,4,40,1]{0,3,1,4,2:T(8,128)(2,1)S(1)}, u32[]{:S(2)}, u32[]{:S(2)}) async-start(bf16[2048,4,4,40,1]{0,3,1,4,2:T(8,128)(2,1)} %copy.39), calls=%async_computation.4 | async-start | bytes 5242880 | tf_op jit(solution)/shard_map/all_to_all | solution.py:71
  301.0 0.0 copy-done.3
  301.0 0.1 copy.30
  301.1 0.6 convolution_bitcast_fusion
  301.7 0.2 copy.31
  302.0 55.3 %all-to-all-done.4 = bf16[2048,4,4,40,1]{0,3,1,4,2:T(8,128)(2,1)S(1)} async-done(((bf16[2048,4,4,40,1]{0,3,1,4,2:T(8,128)(2,1)}), bf16[2048,4,4,40,1]{0,3,1,4,2:T(8,128)(2,1)S(1)}, u32[]{:S(2)}, u32[]{:S(2)}) %all-to-all-start.4) | async-done | bytes 2621472 | tf_op jit(solution)/shard_map/all_to_all | solution.py:71
  357.3 0.0 copy-start.1
  357.3 0.2 copy.40
  357.5 2.3 convolution_convert_fusion.3
  359.7 0.0 copy-done.1
  (1 shorter events, 0.0 us)
Async XLA Ops:
  6.5 3.2 copy-start
  6.5 178.8 %all-gather.3.cloned.1.call-start = ((), (), s32[]{:S(2)}) async-start(), calls=%async_computation.5 | async-start | bytes 7864320 | tf_op jit(solution)/shard_map/all_gather | solution.py:51
  161.5 74.7 %all-to-all-start.2 = ((bf16[2,2,524288]{2,1,0:T(2,128)(2,1)}), bf16[2,2,524288]{2,1,0:T(2,128)(2,1)}, u32[]{:S(2)}, u32[]{:S(2)}) async-start(bf16[2,2,524288]{2,1,0:T(2,128)(2,1)} %reshape.119), calls=%async_computation.2 | async-start | bytes 8388608 | tf_op jit(solution)/shard_map/all_to_all | solution.py:55
  167.1 89.1 %all-gather.5.cloned.1.call-start = ((), (), s32[]{:S(2)}) async-start(), calls=%async_computation.6 | async-start | bytes 1966080 | tf_op jit(solution)/shard_map/all_gather | solution.py:58
  185.3 6.2 %copy-start.4 = (bf16[640,1,4096]{2,0,1:T(8,128)(2,1)S(1)}, bf16[640,1,4096]{2,0,1:T(8,128)(2,1)}, u32[]{:S(2)}) copy-start(bf16[640,1,4096]{2,0,1:T(8,128)(2,1)} %all-gather.3.cloned.1.call-done) | copy-start | bytes 15728644
  185.3 6.5 %copy-start.5 = (bf16[1,4096,512]{2,1,0:T(8,128)(2,1)S(1)}, bf16[1,4096,512]{2,1,0:T(8,128)(2,1)}, u32[]{:S(2)}) copy-start(bf16[1,4096,512]{2,1,0:T(8,128)(2,1)} %param.10) | copy-start | bytes 12582916
  256.2 3.5 copy-start.2
  256.2 3.5 copy-start.6
  295.8 5.3 %copy-start.3 = (f32[64,8]{0,1:T(8,128)S(1)}, f32[64,8]{0,1:T(8,128)}, u32[]{:S(2)}) copy-start(f32[64,8]{0,1:T(8,128)} %param.8) | copy-start | bytes 6148
  295.8 61.5 %all-to-all-start.4 = ((bf16[2048,4,4,40,1]{0,3,1,4,2:T(8,128)(2,1)}), bf16[2048,4,4,40,1]{0,3,1,4,2:T(8,128)(2,1)S(1)}, u32[]{:S(2)}, u32[]{:S(2)}) async-start(bf16[2048,4,4,40,1]{0,3,1,4,2:T(8,128)(2,1)} %copy.39), calls=%async_computation.4 | async-start | bytes 5242880 | tf_op jit(solution)/shard_map/all_to_all | solution.py:71
  357.3 2.4 copy-start.1
Sparse Core Ops, SparseCore 0:
  107.5 77.7 all-gather.2
  195.8 38.1 all-gather.4
where the time goes:
time: 373 us; the launch traced here: 367 us
  blocking collectives  127 us (34%)
  waiting for transfers between devices  114 us (31%)
  local copies, waits for them, and re-layouts  51.4 us (14%)
  other arithmetic  30 us (8%)
  matrix products  19.2 us (5%)
  between operations  13.5 us (4%)
  starting transfers between devices  11.1 us (3%)
    all_to_all x1, blocking collectives, local(): lax.all_to_all(lax.all_to_all(outgoing, 'uly', split_axis=0, concat_axis=...  62 us
    all_to_all x1, waiting for transfers between devices, local(): lax.all_to_all(lax.all_to_all(returned, 'uly', split_axis=1, concat_axis=...  55.3 us
    all_to_all x1, waiting for transfers between devices, local(): lax.all_to_all(w_down, 'blk', split_axis=2, concat_axis=1, tiled=True)  40.6 us
    unnamed x21, local copies, waits for them, and re-layouts  40.5 us
    all_to_all x1, blocking collectives, local(): lax.all_to_all(outgoing, 'uly', split_axis=0, concat_axis=0, tiled=True)  32.7 us
    all_to_all x1, blocking collectives, local(): lax.all_to_all(returned, 'uly', split_axis=1, concat_axis=1, tiled=True)  32.7 us
    unnamed x1, other arithmetic  28.5 us
    all_gather x1, waiting for transfers between devices, local(): portion = lax.all_gather(arrived, 'blk', axis=2, tiled=True)  18 us
  transfers between devices with their start and end apart: 4, of which 3 were waited for; matrix products, arithmetic and copies ran while one was open for 23% of the time, Pallas kernels for 0%

commit v1 on v0

--- a/solution.py
+++ b/solution.py
@@ -22,7 +22,7 @@
     return (placing.astype(jnp.bfloat16), mixing)
 
 
-def local(tokens, expert_ids, route_weight, w_gate, w_up, w_down):
+def local_slots(tokens, expert_ids, route_weight, w_gate, w_up, w_down):
     ulysses_size = lax.axis_size("uly")
     data_size = lax.axis_size("dp")
     cycle_size = lax.axis_size("blk")
@@ -82,9 +82,32 @@
     return mixed.astype(jnp.bfloat16)
 
 
+def local_dense(tokens, expert_ids, route_weight, w_gate, w_up, w_down):
+    data_size = lax.axis_size("dp")
+    local_count = w_gate.shape[0]
+    groups = lax.axis_size("uly") * data_size
+    experts = groups * local_count
+    labels = lax.broadcasted_iota(jnp.int32, (1, 1, experts), 2)
+    scaled = jnp.sum(jnp.where(expert_ids[:, :, None] == labels, route_weight[:, :, None], 0.0), axis=1)
+    everyone = lax.all_gather(tokens, ("uly", "dp"), axis=0, tiled=True)
+    shares = lax.all_gather(scaled, ("uly", "dp"), axis=0, tiled=True)
+    first = (lax.axis_index("uly") * data_size + lax.axis_index("dp")) * local_count
+    total = None
+    for number in range(local_count):
+        share = lax.dynamic_slice_in_dim(shares, first + number, 1, 1)
+        gate = jnp.dot(everyone, w_gate[number], preferred_element_type=jnp.float32)
+        up = jnp.dot(everyone, w_up[number], preferred_element_type=jnp.float32)
+        hidden = (jax.nn.silu(gate) * up * share).astype(jnp.bfloat16)
+        part = jnp.dot(hidden, w_down[number], preferred_element_type=jnp.float32)
+        total = part if total is None else total + part
+    halves = lax.psum_scatter(total.astype(jnp.bfloat16), "blk", scatter_dimension=1, tiled=True)
+    return lax.psum_scatter(halves, ("uly", "dp"), scatter_dimension=0, tiled=True)
+
+
 def solution(mesh):
+    groups = mesh.shape["uly"] * mesh.shape["dp"]
     return jax.shard_map(
-        local,
+        local_dense if groups <= 16 else local_slots,
         mesh=mesh,
         in_specs=(
             P(("uly", "dp"), None),

time: 373 us -> 294 us (0.79)
  waiting for transfers between devices: 114 us -> 221 us
  blocking collectives: 127 us -> 31.3 us
  local copies, waits for them, and re-layouts: 51.4 us -> 0.15 us
  other arithmetic: 30 us -> 0.72 us
  starting transfers between devices: 11.1 us -> 0.08 us
  matrix products: 19.2 us -> 24.1 us
    reduce_scatter x0 -> x2, waiting for transfers between devices: none -> 175 us  [the longest x1 99.5 us: local_dense(): lax.psum_scatter(total.astype(jnp.bfloat16), 'blk', scatter_dimension=1,...]
    all_to_all x3 -> x0, blocking collectives: 127 us -> none  [the longest x1 62 us: local(): lax.all_to_all(lax.all_to_all(outgoing, 'uly', split_axis=0, concat_axis=...]
    all_to_all x2 -> x0, waiting for transfers between devices: 95.9 us -> none  [the longest x1 55.3 us: local(): lax.all_to_all(lax.all_to_all(returned, 'uly', split_axis=1, concat_axis=...]
    unnamed x21 -> x1, local copies, waits for them, and re-layouts: 40.5 us -> 0.1 us
    all_gather x0 -> x1, blocking collectives: none -> 31.3 us  [local_dense(): shares = lax.all_gather(scaled, ('uly', 'dp'), axis=0, tiled=True)]
    unnamed x1 -> x0, other arithmetic: 28.5 us -> none
    all_gather x2 -> x1, waiting for transfers between devices: 18 us -> 45.5 us  [local_dense(): everyone = lax.all_gather(tokens, ('uly', 'dp'), axis=0, tiled=True)]
    all_to_all x2 -> x0, starting transfers between devices: 10.8 us -> none  [the longest x1 5.58 us: local(): lax.all_to_all(w_down, 'blk', split_axis=2, concat_axis=1, tiled=True)]
  transfers between devices with their start and end apart: 4 -> 3, of which waited for: 3 -> 3; matrix products, arithmetic and copies ran while one was open for 23% -> 0% of each run, Pallas kernels for 0% -> 0%
where the time goes in v1:
time: 294 us; the launch traced here: 291 us
  waiting for transfers between devices  221 us (75%)
  blocking collectives  31.3 us (11%)
  matrix products  24.1 us (8%)
  between operations  13.1 us (4%)
    reduce_scatter x1, waiting for transfers between devices, local_dense(): lax.psum_scatter(total.astype(jnp.bfloat16), 'blk', scatter_dimension=1,...  99.5 us
    reduce_scatter x1, waiting for transfers between devices, local_dense(): lax.psum_scatter(halves, ('uly', 'dp'), scatter_dimension=0, tiled=True)  75.7 us
    all_gather x1, waiting for transfers between devices, local_dense(): everyone = lax.all_gather(tokens, ('uly', 'dp'), axis=0, tiled=True)  45.5 us
    all_gather x1, blocking collectives, local_dense(): shares = lax.all_gather(scaled, ('uly', 'dp'), axis=0, tiled=True)  31.3 us
    dot_general x1, matrix products, local_dense(): part = jnp.dot(hidden, w_down[number], preferred_element_type=jnp.float32)  16 us
    dot_general x1, matrix products, local_dense(): gate = jnp.dot(everyone, w_gate[number], preferred_element_type=jnp.float32)  8.14 us
  transfers between devices with their start and end apart: 3, of which 3 were waited for; matrix products, arithmetic and copies ran while one was open for 0% of the time, Pallas kernels for 0%

profile of v1, /device:TPU:18, one launch (start us, length us, event | category | flops | bytes accessed | tf_op | source)
XLA Modules:
  0.0 290.9 jit_solution(17746111028157414352)
XLA Ops:
  6.5 0.0 all-gather.3.cloned.1.call-start
  6.5 0.7 all-gather.3.cloned.1.call-update
  7.3 0.0 reduce-scatter.3.cloned.1.call-start
  7.3 0.7 select_reduce_fusion
  8.0 31.3 %all-gather = f32[16,64,16]{1,2,0:T(8,128)S(1)} all-gather(f32[1,64,16]{1,2,0:T(8,128)S(1)} %bitcast.19), channel_id=1, replica_groups=mesh['blk'=2,'uly'=4,'dp'=4] {'uly','dp'}, dimensions={0}, use_global_device_ids=true | all-gather | bytes 69632 | tf_op jit(solution)/shard_map/all_gather | solution.py:93
  39.3 0.1 reshape.3
  39.5 45.5 %all-gather.3.cloned.1.call-done = bf16[1024,4096]{1,0:T(8,128)(2,1)} async-done(((bf16[64,4096]{1,0:T(8,128)(2,1)}), bf16[1024,4096]{1,0:T(8,128)(2,1)}) %all-gather.3.cloned.1.call-update) | async-done | bytes 8388624 | tf_op jit(solution)/shard_map/all_gather | solution.py:92
  85.0 8.1 %fusion.3 = f32[1024,512]{1,0:T(8,128)S(1)} fusion(bf16[1024,4096]{1,0:T(8,128)(2,1)} %all-gather.3.cloned.1.call-done, bf16[1,4096,512]{2,1,0:T(8,128)(2,1)} %param.9), kind=kOutput, calls=%fused_computation.4 | convolution fusion | flops 4294967296 | bytes 14680064 | tf_op jit(solution)/shard_map/dot_general | solution.py:98
  93.2 16.0 %convolution_convert_fusion = bf16[1024,4096]{1,0:T(8,128)(2,1)} fusion(bf16[1,512,4096]{2,1,0:T(8,128)(2,1)} %param.11, f32[1024,512]{1,0:T(8,128)S(1)} %fusion.3, bf16[1024,4096]{1,0:T(8,128)(2,1)} %all-gather.3.cloned.1.call-done, bf16[1,4096,512]{2,1,0:T(8,128)(2,1)} %param.10, f32[1024]{0:T(1024)S(1)} %bitcast.20), kind=kOutput, calls=%fused_computation | convolution fusion | flops 8597798912 | bytes 27267072 | tf_op jit(solution)/shard_map/dot_general | solution.py:101
  109.1 0.0 reduce-scatter.3.cloned.1.call-update
  109.2 0.0 reduce-scatter.5.cloned.1.call-start
  109.2 99.5 %reduce-scatter.3.cloned.1.call-done = bf16[1024,2048]{1,0:T(8,128)(2,1)} async-done(((bf16[1024,4096]{1,0:T(8,128)(2,1)}), bf16[1024,2048]{1,0:T(8,128)(2,1)}) %reduce-scatter.3.cloned.1.call-update) | async-done | bytes 4194320 | tf_op jit(solution)/shard_map/reduce_scatter | solution.py:103
  208.7 0.0 reduce-scatter.5.cloned.1.call-update
  208.7 75.7 %reduce-scatter.5.cloned.1.call-done = bf16[64,2048]{1,0:T(8,128)(2,1)} async-done(((bf16[1024,2048]{1,0:T(8,128)(2,1)}), bf16[64,2048]{1,0:T(8,128)(2,1)}) %reduce-scatter.5.cloned.1.call-update) | async-done | bytes 262160 | tf_op jit(solution)/shard_map/reduce_scatter | solution.py:104
  (2 shorter events, 0.1 us)
Async XLA Ops:
  6.5 78.5 %all-gather.3.cloned.1.call-start = ((), (), s32[]{:S(2)}) async-start(), calls=%async_computation.2 | async-start | bytes 8912896 | tf_op jit(solution)/shard_map/all_gather | solution.py:92
  7.3 201.4 %reduce-scatter.3.cloned.1.call-start = ((), (), s32[]{:S(2)}) async-start(), calls=%async_computation.3 | async-start | bytes 12582912 | tf_op jit(solution)/shard_map/reduce_scatter | solution.py:103
  109.2 175.3 %reduce-scatter.5.cloned.1.call-start = ((), (), s32[]{:S(2)}) async-start(), calls=%async_computation.4 | async-start | bytes 4456448 | tf_op jit(solution)/shard_map/reduce_scatter | solution.py:104
Sparse Core Ops, SparseCore 0:
  9.5 75.4 all-gather.2
  109.3 99.3 reduce-scatter.2
  212.6 71.8 reduce-scatter.4

commit v2 on v0

--- a/solution.py
+++ b/solution.py
@@ -1,6 +1,8 @@
 import jax
 import jax.numpy as jnp
 from jax import lax
+from jax.experimental import pallas as pl
+from jax.experimental.pallas import tpu as pltpu
 from jax.sharding import PartitionSpec as P
 
 
@@ -22,7 +24,7 @@
     return (placing.astype(jnp.bfloat16), mixing)
 
 
-def local(tokens, expert_ids, route_weight, w_gate, w_up, w_down):
+def local_slots(tokens, expert_ids, route_weight, w_gate, w_up, w_down):
     ulysses_size = lax.axis_size("uly")
     data_size = lax.axis_size("dp")
     cycle_size = lax.axis_size("blk")
@@ -82,9 +84,364 @@
     return mixed.astype(jnp.bfloat16)
 
 
+MESH = pl.DeviceIdType.MESH
+
+
+def neighbours(deep):
+    at_y, at_u, at_z = lax.axis_index("blk"), lax.axis_index("uly"), lax.axis_index("dp")
+    at_x, core = at_u // 2, at_u % 2
+    devices = {
+        "up": {"dp": jnp.minimum(at_z + 1, deep - 1)},
+        "down": {"dp": jnp.maximum(at_z - 1, 0)},
+        "x": {"uly": (1 - at_x) * 2 + core},
+        "y": {"blk": 1 - at_y},
+        "core": {"uly": at_x * 2 + 1 - core},
+    }
+    return at_x, at_y, at_z, core, devices
+
+
+def greet(deep, at_z, devices):
+    barrier = pltpu.get_barrier_semaphore()
+    for name in ("x", "y", "core"):
+        pl.semaphore_signal(barrier, inc=1, device_id=devices[name], device_id_type=MESH)
+
+    @pl.when(at_z > 0)
+    def _():
+        pl.semaphore_signal(barrier, inc=1, device_id=devices["down"], device_id_type=MESH)
+
+    @pl.when(at_z < deep - 1)
+    def _():
+        pl.semaphore_signal(barrier, inc=1, device_id=devices["up"], device_id_type=MESH)
+
+    beside = (at_z > 0).astype(jnp.int32) + (at_z < deep - 1).astype(jnp.int32)
+    pl.semaphore_wait(barrier, 3 + beside)
+
+
+def gather_kernel(deep, parts, apart, tok, own_share, every, shares, own_sem, send, recv):
+    at_x, at_y, at_z, core, devices = neighbours(deep)
+    rows_each, width = tok.shape
+    piece = rows_each // parts
+    plane = width - apart
+    plane_cols = pl.ds(pl.multiple_of(at_y * apart, 128), plane)
+    theirs = pl.ds(pl.multiple_of(at_y * plane, 128), apart)
+    lacking = pl.ds(pl.multiple_of((1 - at_y) * plane, 128), apart)
+    entire = pl.ds(0, width)
+    pending = []
+
+    def group(x_of, core_of, z_of):
+        return (2 * x_of + core_of) * deep + z_of
+
+    def block(x_of, core_of, z_of, k, cols):
+        start = pl.multiple_of(group(x_of, core_of, z_of) * rows_each + k * piece, piece)
+        return every.at[pl.ds(start, piece), cols]
+
+    def copy(src, dst, kind, index, to):
+        return pltpu.make_async_remote_copy(
+            src_ref=src, dst_ref=dst, send_sem=send.at[kind, index], recv_sem=recv.at[kind, index],
+            device_id=devices[to], device_id_type=MESH)
+
+    def start(condition, src, dst, kind, index, to):
+        def go():
+            copy(src, dst, kind, index, to).start()
+
+        if condition is None:
+            go()
+        else:
+            pl.when(condition)(go)
+        pending.append((condition, src, dst, kind, index, to))
+
+    def arrive(dst, kind, index):
+        copy(dst, dst, kind, index, "x").wait_recv()
+
+    greet(deep, at_z, devices)
+    low, high = at_z > 0, at_z < deep - 1
+    mine_at = pl.multiple_of(group(at_x, core, at_z) * rows_each, rows_each)
+    placed = pltpu.make_async_copy(tok, every.at[pl.ds(mine_at, rows_each)], own_sem.at[0])
+    placed.start()
+    share_at = shares.at[group(at_x, core, at_z)]
+    share_placed = pltpu.make_async_copy(own_share, share_at, own_sem.at[1])
+    share_placed.start()
+    for k in range(parts):
+        here = at_z * parts + k
+        source = tok.at[pl.ds(k * piece, piece), plane_cols]
+        target = block(at_x, core, at_z, k, plane_cols)
+        start(high, source, target, 0, here, "up")
+        start(low, source, target, 1, here, "down")
+        start(None, source, target, 2, here, "x")
+    start(high, own_share, share_at, 9, at_z, "up")
+    start(low, own_share, share_at, 10, at_z, "down")
+    start(None, own_share, share_at, 11, at_z, "x")
+    for k in range(parts):
+        start(None, tok.at[pl.ds(k * piece, piece)], block(at_x, core, at_z, k, entire), 5, at_z * parts + k, "core")
+    start(None, own_share, share_at, 12, at_z, "core")
+
+    def from_z(condition, onward, kind, to, z_of, k):
+        held = block(at_x, core, z_of, k, plane_cols)
+        index = z_of * parts + k
+        pl.when(condition)(lambda: arrive(held, kind, index))
+        start(condition & onward, held, held, kind, index, to)
+        start(condition, held, held, 2, index, "x")
+        sent = block(at_x, core, z_of, k, theirs)
+        start(condition, sent, sent, 3, index, "y")
+        start(condition, held, held, 5, index, "core")
+        if k == parts - 1:
+            share = shares.at[group(at_x, core, z_of)]
+            pl.when(condition)(lambda: arrive(share, kind + 9, z_of))
+            start(condition & onward, share, share, kind + 9, z_of, to)
+            start(condition, share, share, 11, z_of, "x")
+            start(condition, share, share, 12, z_of, "core")
+
+    def from_x(condition, z_of, k):
+        held = block(1 - at_x, core, z_of, k, plane_cols)
+        index = z_of * parts + k
+        sent = block(1 - at_x, core, z_of, k, theirs)
+        pl.when(condition)(lambda: arrive(held, 2, index))
+        start(condition, sent, sent, 4, index, "y")
+        start(condition, held, held, 6, index, "core")
+        if k == parts - 1:
+            share = shares.at[group(1 - at_x, core, z_of)]
+            pl.when(condition)(lambda: arrive(share, 11, z_of))
+            start(condition, share, share, 13, z_of, "core")
+
+    def below(step):
+        return at_z >= step, jnp.maximum(at_z - step, 0)
+
+    def above(step):
+        return at_z + step < deep, jnp.minimum(at_z + step, deep - 1)
+
+    def sides(step):
+        return [(at_z >= 0, at_z)] if step == 0 else [below(step), above(step)]
+
+    for step in range(1, deep + 1):
+        for k in range(parts):
+            if step < deep:
+                there, z_of = below(step)
+                from_z(there, high, 0, "up", z_of, k)
+                there, z_of = above(step)
+                from_z(there, low, 1, "down", z_of, k)
+            for there, z_of in sides(step - 1):
+                from_x(there, z_of, k)
+
+    def from_y(condition, x_of, kind, z_of, k):
+        held = block(x_of, core, z_of, k, lacking)
+        index = z_of * parts + k
+        pl.when(condition)(lambda: arrive(held, kind, index))
+        start(condition, held, held, kind + 4, index, "core")
+
+    def each_remote(act):
+        for step in range(deep):
+            for k in range(parts):
+                for there, z_of in sides(step):
+                    if step > 0:
+                        act(there, at_x, 3, z_of, k)
+                    act(there, 1 - at_x, 4, z_of, k)
+
+    each_remote(from_y)
+
+    def from_core(condition, x_of, kind, z_of, k):
+        index = z_of * parts + k
+
+        @pl.when(condition)
+        def _():
+            arrive(block(x_of, 1 - core, z_of, k, plane_cols), kind + 2, index)
+            arrive(block(x_of, 1 - core, z_of, k, lacking), kind + 4, index)
+            if k == parts - 1:
+                arrive(shares.at[group(x_of, 1 - core, z_of)], kind + 9, z_of)
+
+    for k in range(parts):
+        arrive(block(at_x, 1 - core, at_z, k, entire), 5, at_z * parts + k)
+    arrive(shares.at[group(at_x, 1 - core, at_z)], 12, at_z)
+    each_remote(from_core)
+    placed.wait()
+    share_placed.wait()
+    for condition, src, dst, kind, index, to in pending:
+        def end(src=src, dst=dst, kind=kind, index=index, to=to):
+            copy(src, dst, kind, index, to).wait_send()
+
+        if condition is None:
+            end()
+        else:
+            pl.when(condition)(end)
+
+
+def gather(tokens, share, groups, deep):
+    rows_each, width = tokens.shape
+    parts = 2
+    apart = width * 3 // 8 // 128 * 128
+    vmem = pl.BlockSpec(memory_space=pltpu.VMEM)
+    return pl.pallas_call(
+        lambda *refs: gather_kernel(deep, parts, apart, *refs),
+        out_shape=(
+            jax.ShapeDtypeStruct((groups * rows_each, width), tokens.dtype),
+            jax.ShapeDtypeStruct((groups,) + share.shape, share.dtype),
+        ),
+        in_specs=[vmem, vmem],
+        out_specs=(vmem, vmem),
+        scratch_shapes=[
+            pltpu.SemaphoreType.DMA((2,)),
+            pltpu.SemaphoreType.DMA((14, deep * parts)),
+            pltpu.SemaphoreType.DMA((14, deep * parts)),
+        ],
+        compiler_params=pltpu.CompilerParams(
+            collective_id=0, has_side_effects=True, vmem_limit_bytes=40 << 20),
+    )(tokens, share)
+
+
+def scatter_kernel(deep, low_half, high_half, out, total, a1, a2, b1, b2, rising, falling, send, recv):
+    at_x, at_y, at_z, core, devices = neighbours(deep)
+    rows_each = out.shape[0]
+    part = rows_each // 2
+    halves = (low_half, high_half)
+    pending = []
+    order = []
+    for number in range((deep + 1) // 2):
+        order += [number] if number == deep - 1 - number else [number, deep - 1 - number]
+
+    def copy(src, dst, kind, index, to):
+        return pltpu.make_async_remote_copy(
+            src_ref=src, dst_ref=dst, send_sem=send.at[kind, index], recv_sem=recv.at[kind, index],
+            device_id=devices[to], device_id_type=MESH)
+
+    def start(condition, *what):
+        def go():
+            copy(*what).start()
+
+        if condition is None:
+            go()
+        else:
+            pl.when(condition)(go)
+        pending.append((condition, what))
+
+    def rows_of(x_of, core_of, z_of):
+        first = ((2 * x_of + core_of) * deep + z_of) * rows_each
+        return pl.ds(pl.multiple_of(first, rows_each), rows_each)
+
+    def added(one, other):
+        return (one.astype(jnp.float32) + other.astype(jnp.float32)).astype(jnp.bfloat16)
+
+    greet(deep, at_z, devices)
+    for z_of in order:
+        for x_of in range(2):
+            for half in range(2):
+                start(None, halves[half].at[rows_of(x_of, 1 - core, z_of)], total.at[z_of, x_of, half],
+                      0, (z_of * 2 + x_of) * 2 + half, "core")
+    upper, lower = pl.ds(0, part), pl.ds(part, part)
+    for z_of in order:
+        for x_of in range(2):
+            for half in range(2):
+                spot = total.at[z_of, x_of, half]
+                copy(spot, spot, 0, (z_of * 2 + x_of) * 2 + half, "core").wait_recv()
+                total[z_of, x_of, half] = added(total[z_of, x_of, half], halves[half][rows_of(x_of, core, z_of), :])
+        start(None, total.at[z_of, :, 1 - at_y, upper], a1.at[z_of], 1, z_of, "y")
+        start(None, total.at[z_of, 1 - at_x, :, lower], b1.at[z_of], 2, z_of, "x")
+
+    def first_stage(z_of):
+        copy(a1.at[z_of], a1.at[z_of], 1, z_of, "y").wait_recv()
+        for x_of in range(2):
+            total[z_of, x_of, at_y, upper] = added(total[z_of, x_of, at_y, upper], a1[z_of, x_of])
+        start(None, total.at[z_of, 1 - at_x, at_y, upper], a2.at[z_of], 3, z_of, "x")
+        copy(b1.at[z_of], b1.at[z_of], 2, z_of, "x").wait_recv()
+        for half in range(2):
+            total[z_of, at_x, half, lower] = added(total[z_of, at_x, half, lower], b1[z_of, half])
+        start(None, total.at[z_of, at_x, 1 - at_y, lower], b2.at[z_of], 4, z_of, "y")
+
+    def second_stage(z_of):
+        copy(a2.at[z_of], a2.at[z_of], 3, z_of, "x").wait_recv()
+        total[z_of, at_x, at_y, upper] = added(total[z_of, at_x, at_y, upper], a2[z_of])
+        copy(b2.at[z_of], b2.at[z_of], 4, z_of, "y").wait_recv()
+        total[z_of, at_x, at_y, lower] = added(total[z_of, at_x, at_y, lower], b2[z_of])
+
+    def third_stage(z_of):
+        for toward, farther, inbound, kind, to in (
+            (at_z < z_of, at_z > 0, rising, 5, "up"),
+            (at_z > z_of, at_z < deep - 1, falling, 6, "down"),
+        ):
+            @pl.when(toward & farther)
+            def _(inbound=inbound, kind=kind, to=to):
+                copy(inbound.at[z_of], inbound.at[z_of], kind, z_of, to).wait_recv()
+                total[z_of, at_x, at_y] = added(total[z_of, at_x, at_y], inbound[z_of])
+
+            start(toward, total.at[z_of, at_x, at_y], inbound.at[z_of], kind, z_of, to)
+
+    for number in range(deep + 2):
+        if number < deep:
+            first_stage(order[number])
+        if 0 <= number - 1 < deep:
+            second_stage(order[number - 1])
+        if 0 <= number - 2 < deep:
+            third_stage(order[number - 2])
+
+    @pl.when(at_z > 0)
+    def _():
+        copy(rising.at[at_z], rising.at[at_z], 5, at_z, "up").wait_recv()
+        total[at_z, at_x, at_y] = added(total[at_z, at_x, at_y], rising[at_z])
+
+    @pl.when(at_z < deep - 1)
+    def _():
+        copy(falling.at[at_z], falling.at[at_z], 6, at_z, "down").wait_recv()
+        total[at_z, at_x, at_y] = added(total[at_z, at_x, at_y], falling[at_z])
+
+    out[...] = total[at_z, at_x, at_y]
+    for condition, what in pending:
+        def end(what=what):
+            copy(*what).wait_send()
+
+        if condition is None:
+            end()
+        else:
+            pl.when(condition)(end)
+
+
+def scatter(low_half, high_half, rows_each, deep):
+    width = low_half.shape[1]
+    part = rows_each // 2
+    kind = low_half.dtype
+    vmem = pl.BlockSpec(memory_space=pltpu.VMEM)
+    return pl.pallas_call(
+        lambda *refs: scatter_kernel(deep, *refs),
+        out_shape=jax.ShapeDtypeStruct((rows_each, width), kind),
+        in_specs=[vmem, vmem],
+        out_specs=vmem,
+        scratch_shapes=[
+            pltpu.VMEM((deep, 2, 2, rows_each, width), kind),
+            pltpu.VMEM((deep, 2, part, width), kind),
+            pltpu.VMEM((deep, part, width), kind),
+            pltpu.VMEM((deep, 2, part, width), kind),
+            pltpu.VMEM((deep, part, width), kind),
+            pltpu.VMEM((deep, rows_each, width), kind),
+            pltpu.VMEM((deep, rows_each, width), kind),
+            pltpu.SemaphoreType.DMA((7, deep * 4)),
+            pltpu.SemaphoreType.DMA((7, deep * 4)),
+        ],
+        compiler_params=pltpu.CompilerParams(
+            collective_id=1, has_side_effects=True, vmem_limit_bytes=48 << 20),
+    )(low_half, high_half)
+
+
+def local_dense(tokens, expert_ids, route_weight, w_gate, w_up, w_down):
+    deep = lax.axis_size("dp")
+    groups = lax.axis_size("uly") * deep
+    rows_each = tokens.shape[0]
+    labels = lax.broadcasted_iota(jnp.int32, (groups, 1, 1), 0)
+    scaled = jnp.sum(jnp.where(expert_ids[None] == labels, route_weight[None], 0.0), axis=2)
+    scaled = jnp.pad(scaled, ((0, 0), (0, -rows_each % 128)))
+    everyone, shares = gather(tokens, scaled, groups, deep)
+    first = lax.axis_index("uly") * deep + lax.axis_index("dp")
+    share = lax.dynamic_slice_in_dim(shares, first, 1, 1)[:, 0, :rows_each].reshape(groups * rows_each, 1)
+    gate = jnp.dot(everyone, w_gate[0], preferred_element_type=jnp.float32)
+    up = jnp.dot(everyone, w_up[0], preferred_element_type=jnp.float32)
+    hidden = (jax.nn.silu(gate) * up * share).astype(jnp.bfloat16)
+    half = w_down.shape[2] // 2
+    low_half = jnp.dot(hidden, w_down[0, :, :half], preferred_element_type=jnp.float32).astype(jnp.bfloat16)
+    high_half = jnp.dot(hidden, w_down[0, :, half:], preferred_element_type=jnp.float32).astype(jnp.bfloat16)
+    return scatter(low_half, high_half, rows_each, deep)
+
+
 def solution(mesh):
+    groups = mesh.shape["uly"] * mesh.shape["dp"]
+    dense = mesh.shape["blk"] == 2 and mesh.shape["uly"] == 4 and groups <= 16
     return jax.shard_map(
-        local,
+        local_dense if dense else local_slots,
         mesh=mesh,
         in_specs=(
             P(("uly", "dp"), None),

time: 373 us -> 132 us (0.35); the launches traced: 367 us -> 132 us
  blocking collectives: 127 us -> 0 us
  waiting for transfers between devices: 114 us -> 0 us
  Pallas kernels: 0 us -> 106 us
  local copies, waits for them, and re-layouts: 51.4 us -> 5.07 us
  other arithmetic: 30 us -> 0.73 us
  between operations: 13.5 us -> 0.1 us
  starting transfers between devices: 11.1 us -> 0 us
    all_to_all x3 -> x0, blocking collectives: 127 us -> none  [the longest x1 62 us: local(): lax.all_to_all(lax.all_to_all(outgoing, 'uly', split_axis=0, concat_axis=...]
    pallas_call x0 -> x2, Pallas kernels: none -> 106 us  [the longest x1 66.4 us: scatter(): pl.pallas_call(lambda *refs: scatter_kernel(deep, *refs), out_shape=jax.S...]
    all_to_all x2 -> x0, waiting for transfers between devices: 95.9 us -> none  [the longest x1 55.3 us: local(): lax.all_to_all(lax.all_to_all(returned, 'uly', split_axis=1, concat_axis=...]
    unnamed x21 -> x11, local copies, waits for them, and re-layouts: 40.5 us -> 4.97 us
    unnamed x1 -> x0, other arithmetic: 28.5 us -> none
    all_gather x2 -> x0, waiting for transfers between devices: 18 us -> none  [the longest x1 18 us: local(): portion = lax.all_gather(arrived, 'blk', axis=2, tiled=True)]
    all_to_all x2 -> x0, starting transfers between devices: 10.8 us -> none  [the longest x1 5.58 us: local(): lax.all_to_all(w_down, 'blk', split_axis=2, concat_axis=1, tiled=True)]
    all_to_all x5 -> x0, local copies, waits for them, and re-layouts: 10.4 us -> none  [the longest x1 6.3 us: local(): lax.all_to_all(w_down, 'blk', split_axis=2, concat_axis=1, tiled=True)]
  transfers between devices with their start and end apart: 4 -> 0, of which waited for: 3 -> 0; matrix products, arithmetic and copies ran while one was open for 23% -> 0% of each run, Pallas kernels for 0% -> 0%
where the time goes in v2:
time: 132 us
  Pallas kernels  106 us (80%)
  matrix products  19.6 us (15%)
  local copies, waits for them, and re-layouts  5.07 us (4%)
    pallas_call x1, Pallas kernels, scatter(): pl.pallas_call(lambda *refs: scatter_kernel(deep, *refs), out_shape=jax.S...  66.4 us
    pallas_call x1, Pallas kernels, gather(): pl.pallas_call(lambda *refs: gather_kernel(deep, parts, apart, *refs), ou...  39.8 us
    dot_general x1, matrix products, local_dense(): gate = jnp.dot(everyone, w_gate[0], preferred_element_type=jnp.float32)  8.27 us
    unnamed x11, local copies, waits for them, and re-layouts  4.97 us
    dot_general x1, matrix products, local_dense(): up = jnp.dot(everyone, w_up[0], preferred_element_type=jnp.float32)  4.75 us
    dot_general x1, matrix products, local_dense(): jnp.dot(hidden, w_down[0, :, half:], preferred_element_type=jnp.float32)  4.28 us

profile of v2, /device:TPU:18, one launch (start us, length us, event | category | flops | bytes accessed | tf_op | source)
XLA Modules:
  0.0 131.7 jit_solution(12932249947474507887)
XLA Ops:
  0.0 0.7 select_reduce_fusion
  0.7 0.0 copy-start
  0.8 1.0 copy-done
  1.8 39.8 %shard_map.64 = (bf16[1024,4096]{1,0:T(8,128)(2,1)S(1)}, f32[16,16,128]{2,1,0:T(8,128)S(1)}) custom-call(bf16[64,4096]{1,0:T(8,128)(2,1)S(1)} %copy-done, f32[16,128]{1,0:T(8,128)S(1)} %pad.4.refs_1_), custom_call_target="tpu_custom_call" | custom-call | tf_op jit(solution)/shard_map/pallas_call | solution.py:272
  41.6 0.0 copy-start.1
  41.6 3.2 %copy-done.1 = bf16[1024,4096]{1,0:T(8,128)(2,1)} copy-done((bf16[1024,4096]{1,0:T(8,128)(2,1)}, bf16[1024,4096]{1,0:T(8,128)(2,1)S(1)}, u32[]{:S(2)}) %copy-start.1) | copy-done | bytes 8388632
  44.8 0.1 mul.23
  44.9 0.0 copy-start.2
  44.9 0.0 copy-start.3
  44.9 8.3 %fusion.2 = f32[1024,512]{1,0:T(8,128)S(1)} fusion(bf16[1024,4096]{1,0:T(8,128)(2,1)} %copy-done.1, bf16[1,4096,512]{2,1,0:T(8,128)(2,1)} %param.9), kind=kOutput, calls=%fused_computation.2 | convolution fusion | flops 4294967296 | bytes 14680064 | tf_op jit(solution)/shard_map/dot_general | solution.py:431
  53.2 0.0 copy-done.2
  53.2 0.0 copy-done.3
  53.2 0.0 copy-start.4
  53.2 4.8 %multiply_convert_fusion = bf16[1024,512]{1,0:T(8,128)(2,1)S(1)} fusion(f32[1024,512]{1,0:T(8,128)S(1)} %fusion.2, bf16[1024,4096]{1,0:T(8,128)(2,1)S(1)} %copy-done.2, bf16[1,4096,512]{2,1,0:T(8,128)(2,1)S(1)} %copy-done.3, f32[1024]{0:T(1024)S(1)} %mul.23), kind=kOutput, calls=%fused_computation.10 | convolution fusion | flops 4298637312 | bytes 15732736 | tf_op jit(solution)/shard_map/dot_general | solution.py:432
  58.0 0.0 copy-done.4
  58.0 4.3 %convolution_convert_fusion.refs_1_ = bf16[1024,2048]{1,0:T(8,128)(2,1)} fusion(bf16[1024,512]{1,0:T(8,128)(2,1)S(1)} %multiply_convert_fusion, bf16[1,512,4096]{2,1,0:T(8,128)(2,1)S(1)} %copy-done.4), kind=kOutput, calls=%fused_computation.4 | convolution fusion | flops 2149580800 | bytes 7340032 | tf_op jit(solution)/shard_map/dot_general | solution.py:436
  62.3 2.3 %convolution_convert_fusion.1.refs_0_ = bf16[1024,2048]{1,0:T(8,128)(2,1)S(1)} fusion(bf16[1024,512]{1,0:T(8,128)(2,1)S(1)} %multiply_convert_fusion, bf16[1,512,4096]{2,1,0:T(8,128)(2,1)S(1)} %copy-done.4), kind=kOutput, calls=%fused_computation.5 | convolution fusion | flops 2149580800 | bytes 7340032 | tf_op jit(solution)/shard_map/dot_general | solution.py:435
  64.6 66.4 %shard_map.65 = bf16[64,2048]{1,0:T(8,128)(2,1)S(1)} custom-call(bf16[1024,2048]{1,0:T(8,128)(2,1)S(1)} %convolution_convert_fusion.1.refs_0_, bf16[1024,2048]{1,0:T(8,128)(2,1)} %convolution_convert_fusion.refs_1_), custom_call_target="tpu_custom_call" | custom-call | tf_op jit(solution)/shard_map/pallas_call | solution.py:400
  131.0 0.7 copy.10
  (2 shorter events, 0.0 us)
Async XLA Ops:
  0.7 1.0 copy-start
  41.6 3.2 %copy-start.1 = (bf16[1024,4096]{1,0:T(8,128)(2,1)}, bf16[1024,4096]{1,0:T(8,128)(2,1)S(1)}, u32[]{:S(2)}) copy-start(bf16[1024,4096]{1,0:T(8,128)(2,1)S(1)} %get-tuple-element.7) | copy-start | bytes 25165828
  44.9 8.3 %copy-start.2 = (bf16[1024,4096]{1,0:T(8,128)(2,1)S(1)}, bf16[1024,4096]{1,0:T(8,128)(2,1)}, u32[]{:S(2)}) copy-start(bf16[1024,4096]{1,0:T(8,128)(2,1)} %copy-done.1) | copy-start | bytes 25165828
  44.9 8.3 %copy-start.3 = (bf16[1,4096,512]{2,1,0:T(8,128)(2,1)S(1)}, bf16[1,4096,512]{2,1,0:T(8,128)(2,1)}, u32[]{:S(2)}) copy-start(bf16[1,4096,512]{2,1,0:T(8,128)(2,1)} %param.10) | copy-start | bytes 12582916
  53.2 4.8 %copy-start.4 = (bf16[1,512,4096]{2,1,0:T(8,128)(2,1)S(1)}, bf16[1,512,4096]{2,1,0:T(8,128)(2,1)}, u32[]{:S(2)}) copy-start(bf16[1,512,4096]{2,1,0:T(8,128)(2,1)} %param.11) | copy-start | bytes 12582916
